TPU v7x, 32 devices: a whole 2x2x4 slice. The times are simulated.
32 devices in a mesh: dp: 4 (over y, x), vocab: 8 (over z, core).
Axes of the slice: x: 2, y: 2, z: 4, core: 2. Of those that a mesh axis runs over, the one named last changes fastest.
Arguments:
- hidden: bfloat16 [1024, 8192], P('dp'), may hold values from -14 to 14
- weight: bfloat16 [8192, 8192], P('dp', 'vocab'), may hold values from -1 to 1, as said below
- targets: int32 [1024], P('dp'), may hold values from 0 to 8191
- cotangent: float32 [1024], P('dp'), may hold values from 1 to 8
Outputs:
- loss: float32 [1024], P('dp')
- grad_hidden: bfloat16 [1024, 8192], P('vocab', 'dp')
- grad_weight: bfloat16 [8192, 8192], P('dp', 'vocab')
Inputs may be any that keep to these rules, and one draw needn't show every extreme that they name: `weight`: entries drawn with standard deviation 4 / sqrt(8192).
All inputs are finite; a program needn't handle non-finite values.
Results may differ from a plain program's by a relative error of at most 0.0047.
Values may be sent and summed in bfloat16 or wider, within the bound.
A program may use at most 128 MiB of HBM per device.

v0:
```python
import functools

import jax
import jax.numpy as jnp
from jax import lax
from jax.experimental import pallas as pl
from jax.experimental.pallas import tpu as pltpu
from jax.sharding import PartitionSpec as P

F32 = jnp.float32
BF16 = jnp.bfloat16
WIRE = jnp.int16
STEPS = 32000.0


def kernel(
    nd, nv, levels,
    h_ref, w_hbm, t_ref, c_ref,
    loss_ref, gh_ref, gw_ref,
    w, spread, logit, psend, precv, stats, grads, acc, sbuf, rbuf, gwbuf, tcol, ccol, col,
    part_f32, usend, urecv, ucol,
    w_sem, own_sem, gw_sem,
    hs_send, hs_recv, hf_send, hf_recv, hx_send, hx_recv, p_send, p_recv, u_send, u_recv,
    st_send, st_recv, g_send, g_recv, x_send, x_recv, r_send, r_recv,
):
    d, v = lax.axis_index("dp"), lax.axis_index("vocab")
    core = lax.rem(v, 2)

    def flip(i, mask):
        for bit in range(mask.bit_length()):
            if mask >> bit & 1:
                i = i + (1 - 2 * lax.rem(i // (1 << bit), 2)) * (1 << bit)
        return i

    mate, across = flip(v, 1), flip(v, 2)
    side = lax.rem(v // 2, 2)
    depth, width = w.shape
    tokens = spread.shape[0]
    rows = tokens // nd
    half = rows // 2
    quarter = rows // 4
    share = tokens // nv
    per = rows // share

    load_w = pltpu.make_async_copy(w_hbm, w, w_sem)
    load_w.start()
    own_rows = pl.ds(pl.multiple_of(d * rows, rows), rows)
    load_own = pltpu.make_async_copy(
        h_ref.at[:, pl.ds(pl.multiple_of(d * depth, depth), depth)], spread.at[own_rows], own_sem
    )
    load_own.start()

    barrier = pltpu.get_barrier_semaphore()
    for k in range(1, nd):
        pl.semaphore_signal(barrier, inc=1, device_id={"dp": flip(d, k)})
    for k in range(1, nv):
        pl.semaphore_signal(barrier, inc=1, device_id={"vocab": lax.rem(v + k, nv)})
    pl.semaphore_wait(barrier, nd + nv - 2)

    def remote(src, dst, send, recv, where):
        return pltpu.make_async_remote_copy(
            src_ref=src, dst_ref=dst, send_sem=send, recv_sem=recv, device_id=where
        )

    def piece(s, q):
        return spread.at[pl.ds(pl.multiple_of(s * rows + q * quarter, quarter), quarter)]

    mine = 2 * side + core
    hidden_sends = []
    for k in range(1, nd):
        to = flip(d, k)
        copy = remote(
            h_ref.at[
                pl.ds(pl.multiple_of(mine * quarter, quarter), quarter),
                pl.ds(pl.multiple_of(to * depth, depth), depth),
            ],
            piece(d, mine), hs_send.at[k - 1], hs_recv.at[k - 1], {"dp": to},
        )
        copy.start()
        hidden_sends.append(copy)

    tcol[...] = jnp.broadcast_to(t_ref[...], (128, rows)).T
    ccol[...] = jnp.broadcast_to(c_ref[...], (128, rows)).T

    tile = min(256, width)
    code_rows = min(32, half)

    def project(first, count, store):
        def step(n, _):
            cols = pl.ds(pl.multiple_of(n * tile, tile), tile)
            store(cols, jnp.dot(
                spread[pl.ds(pl.multiple_of(first, count), count), :], w[:, cols],
                preferred_element_type=F32,
            ))
            return 0

        lax.fori_loop(0, width // tile, step, 0)

    load_w.wait()
    load_own.wait()

    def store_own(cols, value):
        logit[:, cols] = value

    project(d * rows, rows, store_own)

    forwards, crossings, partial_sends = [], [], []
    for turn in range(2):
        for k in range(1, nd):
            s = flip(d, k)
            part = side if turn == 0 else 1 - side
            got = piece(s, 2 * part + core)
            to_mate = remote(got, got, hf_send.at[k - 1, turn], hf_recv.at[k - 1, turn], {"vocab": mate})
            over = remote(got, got, hx_send.at[k - 1], hx_recv.at[k - 1], {"vocab": across})
            if turn == 0:
                remote(got, got, hs_send.at[k - 1], hs_recv.at[k - 1], {"dp": s}).wait_recv()
                over.start()
                crossings.append(over)
            else:
                over.wait_recv()
            to_mate.start()
            forwards.append(to_mate)
            to_mate.wait_recv()
            there = pl.ds(pl.multiple_of(part * half, half), half)

            def store_part(cols, value):
                part_f32[:, cols] = value

            project(s * rows + part * half, half, store_part)

            def encode(i, _, k=k, part=part):
                at = pl.ds(pl.multiple_of(i * code_rows, code_rows), code_rows)
                x = part_f32[at, :]
                unit = jnp.maximum(jnp.max(jnp.abs(x), axis=1, keepdims=True), 1e-30) / STEPS
                there = pl.ds(pl.multiple_of(part * half + i * code_rows, code_rows), code_rows)
                psend[k - 1, there, :] = jnp.round(x / unit).astype(jnp.int32).astype(WIRE)
                col[at, :] = jnp.broadcast_to(unit, (code_rows, 128))
                return 0

            lax.fori_loop(0, half // code_rows, encode, 0)
            usend[k - 1, turn] = col[:half, :].T[:8, :]
            for copy in (
                remote(
                    psend.at[k - 1, there], precv.at[k - 1, there],
                    p_send.at[k - 1, turn], p_recv.at[k - 1, turn], {"dp": s},
                ),
                remote(
                    usend.at[k - 1, turn], urecv.at[k - 1, turn],
                    u_send.at[k - 1, turn], u_recv.at[k - 1, turn], {"dp": s},
                ),
            ):
                copy.start()
                partial_sends.append(copy)
    for copy in partial_sends:
        copy.wait_recv()
    for k in range(1, nd):
        for turn in range(2):
            part = side if turn == 0 else 1 - side
            there = pl.ds(pl.multiple_of(part * half, half), half)
            ucol[k - 1, there, :] = jnp.broadcast_to(urecv[k - 1, turn][0:1, :], (128, half)).T

    step_rows = min(32, rows)
    column = lax.broadcasted_iota(jnp.int32, (step_rows, width), 1) + v * width
    lane = lax.broadcasted_iota(jnp.int32, (step_rows, 128), 1)

    def measure(i, _):
        at = pl.ds(pl.multiple_of(i * step_rows, step_rows), step_rows)
        x = logit[at, :]
        for k in range(1, nd):
            x = x + precv[k - 1, at, :].astype(jnp.int32).astype(F32) * ucol[k - 1, at, :1]
        top = jnp.max(x, axis=1, keepdims=True)
        e = jnp.exp(x - top)
        total = jnp.sum(e, axis=1, keepdims=True)
        pick = jnp.sum(jnp.where(column == tcol[at, :1], x, 0.0), axis=1, keepdims=True)
        logit[at, :] = e
        col[at, :] = jnp.where(lane == 0, top, jnp.where(lane == 1, total, pick))
        return 0

    lax.fori_loop(0, rows // step_rows, measure, 0)
    stats[v] = col[...].T[:8, :]
    stat_sends = []
    for k in range(1, nv):
        copy = remote(
            stats.at[v], stats.at[v], st_send.at[k - 1], st_recv.at[k - 1],
            {"vocab": lax.rem(v + k, nv)},
        )
        copy.start()
        stat_sends.append(copy)
    own_top = stats[v][0:1, :]
    for copy in stat_sends:
        copy.wait_recv()
    top = stats[0][0:1, :]
    for u in range(1, nv):
        top = jnp.maximum(top, stats[u][0:1, :])
    total = jnp.zeros_like(top)
    pick = jnp.zeros_like(top)
    for u in range(nv):
        block = stats[u]
        total = total + block[1:2, :] * jnp.exp(block[0:1, :] - top)
        pick = pick + block[2:3, :]
    loss_ref[...] = top + jnp.log(total) - pick
    scale = c_ref[...] * jnp.exp(own_top - top) / total
    col[...] = jnp.broadcast_to(scale, (128, rows)).T

    def differentiate(i, _):
        at = pl.ds(pl.multiple_of(i * step_rows, step_rows), step_rows)
        onehot = jnp.where(column == tcol[at, :1], ccol[at, :1], 0.0)
        g = logit[at, :] * col[at, :1] - onehot
        grads[pl.ds(pl.multiple_of(d * rows + i * step_rows, step_rows), step_rows), :] = g.astype(BF16)
        return 0

    lax.fori_loop(0, rows // step_rows, differentiate, 0)
    relayed = nd == 4
    grad_sends = []
    for k in range(1, nd - 1 if relayed else nd):
        copy = remote(
            grads.at[own_rows], grads.at[own_rows], g_send.at[k - 1], g_recv.at[k - 1],
            {"dp": flip(d, k)},
        )
        copy.start()
        grad_sends.append(copy)

    def relay(k):
        block = grads.at[pl.ds(pl.multiple_of(flip(d, k) * rows + (k - 1) * half, half), half)]
        return remote(block, block, x_send.at[k - 1], x_recv.at[k - 1], {"dp": flip(d, 3 - k)})

    relays = [relay(1), relay(2)] if relayed else []

    depth_tile = min(256, depth)

    def pull(k):
        s = flip(d, k)

        def step(n, _):
            at = pl.ds(pl.multiple_of(n * depth_tile, depth_tile), depth_tile)
            value = lax.dot_general(
                grads[pl.ds(pl.multiple_of(s * rows, rows), rows), :], w[at, :],
                (((1,), (1,)), ((), ())), preferred_element_type=F32,
            )
            for j in range(per):
                acc[k * per + j, :, at] = value[j * share:(j + 1) * share, :]
            return 0

        lax.fori_loop(0, depth // depth_tile, step, 0)

    def ahead(b):
        s = flip(d, b // per)
        return s * per + b % per - v + nv

    def partner(level):
        bit = lax.rem(v // (1 << level), 2)
        return {"vocab": v + (1 - 2 * bit) * (1 << level)}

    chunk = min(16, share)

    cuts = 2
    span = depth // cuts

    def hop(b, level, q):
        at = pl.ds(q * span, span)
        return remote(
            sbuf.at[b, :, at], rbuf.at[level, b, :, at], r_send.at[b, q], r_recv.at[level, b, q], partner(level)
        )

    def each_chunk(body):
        def step(i, _):
            body(pl.ds(pl.multiple_of(i * chunk, chunk), chunk))
            return 0

        lax.fori_loop(0, share // chunk, step, 0)

    def send(b, level, q):
        mine = lax.rem(ahead(b), 1 << level) == 0
        leaves = lax.rem(ahead(b), 2 << level) != 0
        cols = pl.ds(q * span, span)

        @pl.when(jnp.logical_and(mine, leaves))
        def _():
            def body(at):
                sbuf[b, at, cols] = acc[b, at, cols].astype(BF16)

            each_chunk(body)
            hop(b, level, q).start()

    def receive(b, level):
        for q in range(cuts):
            cols = pl.ds(q * span, span)

            @pl.when(lax.rem(ahead(b), 2 << level) == 0)
            def _(q=q, cols=cols):
                hop(b, level, q).wait_recv()

                def body(at):
                    acc[b, at, cols] = acc[b, at, cols] + rbuf[level, b, at, cols].astype(F32)

                each_chunk(body)

            if level + 1 < levels:
                send(b, level + 1, q)

    def arrive(k):
        if relayed and k == nd - 1:
            for copy in relays:
                copy.wait_recv()
        elif k:
            grad_sends[k - 1].wait_recv()
            if relayed:
                relays[k - 1].start()

    pending = []
    for k in range(nd):
        if relayed and k == 1:
            arrive(1)
            arrive(2)
        elif not (relayed and k == 2):
            arrive(k)
        pull(k)
        for j in range(per):
            for q in range(cuts):
                send(k * per + j, 0, q)
        for j in range(per):
            receive(k * per + j, 0)
            pending.append(k * per + j)
        if k >= 2 and levels > 1:
            for b in pending[:per]:
                receive(b, 1)
            pending = pending[per:]

    def weigh(n, _):
        at = pl.ds(pl.multiple_of(n * depth_tile, depth_tile), depth_tile)
        gwbuf[at, :] = lax.dot_general(
            spread[:, at], grads[...], (((0,), (0,)), ((), ())), preferred_element_type=F32
        ).astype(BF16)
        pltpu.make_async_copy(gwbuf.at[at], gw_ref.at[at], gw_sem.at[n]).start()
        return 0

    lax.fori_loop(0, depth // depth_tile, weigh, 0)

    for level in range(1, levels):
        for b in pending if level == 1 else range(nv):
            receive(b, level)
    for b in range(nv):
        @pl.when(ahead(b) == nv)
        def _(b=b):
            def body(at):
                gh_ref[at, :] = acc[b, at, :].astype(BF16)

            each_chunk(body)

        @pl.when(ahead(b) != nv)
        def _(b=b):
            for q in range(cuts):
                hop(b, 0, q).wait_send()

    for copy in hidden_sends + forwards + crossings + partial_sends + stat_sends + grad_sends + relays:
        copy.wait_send()
    for n in range(depth // depth_tile):
        at = pl.ds(n * depth_tile, depth_tile)
        pltpu.make_async_copy(gwbuf.at[at], gw_ref.at[at], gw_sem.at[n]).wait()


def shards(nd, nv, hidden, weight, targets, cotangent):
    rows = hidden.shape[0]
    tokens = rows * nd
    depth, width = weight.shape
    share = tokens // nv
    levels = nv.bit_length() - 1
    dma = pltpu.SemaphoreType.DMA
    vmem = pl.BlockSpec(memory_space=pltpu.VMEM)
    anywhere = pl.BlockSpec(memory_space=pl.ANY)
    flops = 6 * tokens * depth * width
    loss, grad_hidden, grad_weight = pl.pallas_call(
        functools.partial(kernel, nd, nv, levels),
        out_shape=(
            jax.ShapeDtypeStruct((1, rows), F32),
            jax.ShapeDtypeStruct((share, depth), BF16),
            jax.ShapeDtypeStruct((depth, width), BF16),
        ),
        in_specs=[anywhere, anywhere, vmem, vmem],
        out_specs=(vmem, vmem, anywhere),
        scratch_shapes=[
            pltpu.VMEM((depth, width), BF16),
            pltpu.VMEM((tokens, depth), BF16),
            pltpu.VMEM((rows, width), F32),
            pltpu.VMEM((nd - 1, rows, width), WIRE),
            pltpu.VMEM((nd - 1, rows, width), WIRE),
            pltpu.VMEM((nv, 8, rows), F32),
            pltpu.VMEM((tokens, width), BF16),
            pltpu.VMEM((nv, share, depth), F32),
            pltpu.VMEM((nv, share, depth), BF16),
            pltpu.VMEM((levels, nv, share, depth), BF16),
            pltpu.VMEM((depth, width), BF16),
            pltpu.VMEM((rows, 128), jnp.int32),
            pltpu.VMEM((rows, 128), F32),
            pltpu.VMEM((rows, 128), F32),
            pltpu.VMEM((rows // 2, width), F32),
            pltpu.VMEM((nd - 1, 2, 8, rows // 2), F32),
            pltpu.VMEM((nd - 1, 2, 8, rows // 2), F32),
            pltpu.VMEM((nd - 1, rows, 128), F32),
            dma, dma, dma((depth // min(256, depth),)),
            dma((nd - 1,)), dma((nd - 1,)), dma((nd - 1, 2)), dma((nd - 1, 2)), dma((nd - 1,)), dma((nd - 1,)),
            dma((nd - 1, 2)), dma((nd - 1, 2)), dma((nd - 1, 2)), dma((nd - 1, 2)),
            dma((nv - 1,)), dma((nv - 1,)),
            dma((nd - 1,)), dma((nd - 1,)),
            dma((2,)), dma((2,)),
            dma((nv, 2)), dma((levels, nv, 2)),
        ],
        compiler_params=pltpu.CompilerParams(
            collective_id=0, has_side_effects=True, vmem_limit_bytes=66_000_000
        ),
        cost_estimate=pl.CostEstimate(flops=flops, bytes_accessed=16 << 20, transcendentals=0),
        name="token_loss",
    )(hidden, weight, targets.reshape(1, rows), cotangent.reshape(1, rows))
    return loss.reshape(rows), grad_hidden, grad_weight


def solution(mesh):
    in_specs = (P("dp", None), P("dp", "vocab"), P("dp"), P("dp"))
    out_specs = (P("dp"), P("vocab", "dp"), P("dp", "vocab"))
    body = functools.partial(shards, mesh.shape["dp"], mesh.shape["vocab"])
    return jax.shard_map(body, mesh=mesh, in_specs=in_specs, out_specs=out_specs, check_vma=False)
```

profile of v0, /device:TPU:7, one launch (start us, length us, event | category | flops | bytes accessed | tf_op | source)
XLA Modules:
  0.0 122.5 jit_solution(16428626686628664743)
XLA Ops:
  0.6 114.1 %token_loss.1 = (f32[1,256]{1,0:T(1,128)}, bf16[128,2048]{1,0:T(8,128)(2,1)}, bf16[2048,1024]{1,0:T(8,128)(2,1)}) custom-call(bf16[256,8192]{1,0:T(8,128)(2,1)} %h_ref.1, bf16[2048,1024]{1,0:T(8,128)(2,1)} %w_hbm.1, s32[1,256]{1,0:T(1,128)} %bitcast.4, f32[1,256]{1,0:T(1,128)} %bitcast.5), custom_call_target="tpu_custom_call" | custom-call | flops 12884901888 | bytes 16777216 | tf_op jit(solution)/shard_map/token_loss/pallas_call | solution.py:372
  114.7 1.2 %copy.10 = f32[256]{0:T(256)} copy(f32[256]{0:T(256)} %bitcast.3) | data formatting | bytes 2048
  115.9 1.9 %copy.11 = bf16[128,2048]{1,0:T(8,128)(2,1)} copy(bf16[128,2048]{1,0:T(8,128)(2,1)} %get-tuple-element.13) | data formatting | bytes 1048576
  117.8 4.6 %copy.12 = bf16[2048,1024]{1,0:T(8,128)(2,1)} copy(bf16[2048,1024]{1,0:T(8,128)(2,1)} %get-tuple-element.14) | data formatting | bytes 8388608
where the time goes:
time: 123 us; the launch traced here: 122 us
  Pallas kernels  114 us (93%)
  local copies, waits for them, and re-layouts  7.75 us (6%)
    pallas_call x1, Pallas kernels, shards(): pl.pallas_call(functools.partial(kernel, nd, nv, levels), out_shape=(jax....  114 us
    unnamed x3, local copies, waits for them, and re-layouts  7.75 us

commit v1 on v0

--- a/solution.py
+++ b/solution.py
@@ -13,7 +13,7 @@
 STEPS = 32000.0
 
 
-def kernel(
+def butterfly_kernel(
     nd, nv, levels,
     h_ref, w_hbm, t_ref, c_ref,
     loss_ref, gh_ref, gw_ref,
@@ -359,7 +359,7 @@
         pltpu.make_async_copy(gwbuf.at[at], gw_ref.at[at], gw_sem.at[n]).wait()
 
 
-def shards(nd, nv, hidden, weight, targets, cotangent):
+def butterfly(nd, nv, hidden, weight, targets, cotangent):
     rows = hidden.shape[0]
     tokens = rows * nd
     depth, width = weight.shape
@@ -370,7 +370,7 @@
     anywhere = pl.BlockSpec(memory_space=pl.ANY)
     flops = 6 * tokens * depth * width
     loss, grad_hidden, grad_weight = pl.pallas_call(
-        functools.partial(kernel, nd, nv, levels),
+        functools.partial(butterfly_kernel, nd, nv, levels),
         out_shape=(
             jax.ShapeDtypeStruct((1, rows), F32),
             jax.ShapeDtypeStruct((share, depth), BF16),
@@ -414,8 +414,465 @@
     return loss.reshape(rows), grad_hidden, grad_weight
 
 
+CHUNKS = 4
+VMEM_GRANT = 58_000_000
+
+
+def chain_kernel(
+    nd, nv, plan,
+    h_ref, w_hbm, t_ref, c_ref,
+    loss_ref, gh_ref, gw_ref,
+    w, spread, part, psend, precv, usend, urecv, stats, grads, acc, xsend, xrecv, zsend, zrecv,
+    tcol, ccol, col, losscol,
+    w_sem, own_sem,
+    hs_send, hs_recv, hx_send, hx_recv, hf_send, hf_recv, p_send, p_recv, u_send, u_recv,
+    st_send, st_recv, g_send, g_recv, r_send, r_recv, x_send, x_recv, z_send, z_recv,
+):
+    d, v = lax.axis_index("dp"), lax.axis_index("vocab")
+    z, core = v // 2, lax.rem(v, 2)
+    chips = nv // 2
+    side = lax.rem(z, 2)
+    depth, width = w.shape
+    chunks, _, count, _ = spread.shape
+    rows = tcol.shape[0]
+    half = rows // 2
+    cr = count // 2
+    qr = count // 4
+    total_rows = nd * count
+
+    def flip(i, mask):
+        for bit in range(mask.bit_length()):
+            if mask >> bit & 1:
+                i = i + (1 - 2 * lax.rem(i // (1 << bit), 2)) * (1 << bit)
+        return i
+
+    def xor(a, b):
+        return lax.rem(a + b, 2) + 2 * lax.rem(a // 2 + b // 2, 2)
+
+    mate, across = flip(v, 1), flip(v, 2)
+
+    def remote(src, dst, send, recv, where):
+        return pltpu.make_async_remote_copy(
+            src_ref=src, dst_ref=dst, send_sem=send, recv_sem=recv, device_id=where
+        )
+
+    load_w = pltpu.make_async_copy(w_hbm, w, w_sem)
+    load_w.start()
+    own_cols = pl.ds(pl.multiple_of(d * depth, depth), depth)
+
+    def own_load(c, h):
+        return pltpu.make_async_copy(
+            h_ref.at[pl.ds(h * half + c * cr, cr), own_cols],
+            spread.at[c, 0, pl.ds(h * cr, cr)], own_sem.at[c, h],
+        )
+
+    for c in range(chunks):
+        for h in range(2):
+            own_load(c, h).start()
+
+    barrier = pltpu.get_barrier_semaphore()
+    for k in range(1, nd):
+        pl.semaphore_signal(barrier, inc=1, device_id={"dp": flip(d, k)})
+    for k in range(1, nv):
+        pl.semaphore_signal(barrier, inc=1, device_id={"vocab": lax.rem(v + k, nv)})
+    pl.semaphore_wait(barrier, nd + nv - 2)
+
+    sent = []
+
+    def go(copy):
+        copy.start()
+        sent.append(copy)
+
+    def hidden_copy(c, k):
+        to = flip(d, k)
+        first = pl.multiple_of(side * half + c * cr + core * qr, qr)
+        return remote(
+            h_ref.at[pl.ds(first, qr), pl.ds(pl.multiple_of(to * depth, depth), depth)],
+            spread.at[c, k, pl.ds(pl.multiple_of((2 * side + core) * qr, qr), qr)],
+            hs_send.at[c, k - 1], hs_recv.at[c, k - 1], {"dp": to},
+        )
+
+    def slab(c, piece):
+        return spread.at[c, pl.ds(1, nd - 1), pl.ds(pl.multiple_of(piece * qr, qr), qr)]
+
+    def across_copy(c):
+        block = slab(c, 2 * side + core)
+        return remote(block, block, hx_send.at[c], hx_recv.at[c], {"vocab": across})
+
+    def mate_copy(c, turn):
+        block = slab(c, 2 * (side if turn == 0 else 1 - side) + core)
+        return remote(block, block, hf_send.at[c, turn], hf_recv.at[c, turn], {"vocab": mate})
+
+    for c in range(chunks):
+        for k in (3, 1, 2):
+            go(hidden_copy(c, k))
+
+    tcol[...] = jnp.broadcast_to(t_ref[...], (128, rows)).T
+    ccol[...] = jnp.broadcast_to(c_ref[...], (128, rows)).T
+    load_w.wait()
+
+    def gather(c):
+        for k in range(1, nd):
+            hidden_copy(c, k).wait_recv()
+        go(across_copy(c))
+        go(mate_copy(c, 0))
+
+    def cross(c):
+        across_copy(c).wait_recv()
+        go(mate_copy(c, 1))
+
+    tile = min(256, width)
+
+    def project(c):
+        for h in range(2):
+            own_load(c, h).wait()
+        for turn in range(2):
+            mate_copy(c, turn).wait_recv()
+
+        def step(n, _):
+            cols = pl.ds(pl.multiple_of(n * tile, tile), tile)
+            value = jnp.dot(
+                spread[c].reshape(total_rows, depth), w[:, cols], preferred_element_type=F32
+            )
+            part[c, :, :, cols] = value.reshape(nd, count, tile)
+            return 0
+
+        lax.fori_loop(0, width // tile, step, 0)
+
+    def encode(c, k, h, x):
+        at = pl.ds(h * cr, cr)
+        top = jnp.maximum(jnp.max(jnp.abs(x), axis=1, keepdims=True), 1e-30)
+        psend[c, k - 1, at, :] = jnp.round(x * (STEPS / top)).astype(jnp.int32).astype(WIRE)
+        col[c, k - 1, at, :] = jnp.broadcast_to(top / STEPS, (cr, 128))
+
+    def part_copy(c, k, h, to, n):
+        at = pl.ds(h * cr, cr)
+        return remote(
+            psend.at[c, k - 1, at], precv.at[c, k - 1, at], p_send.at[c, n], p_recv.at[c, n], {"dp": flip(d, to)}
+        )
+
+    def unit_copy(c, k, n):
+        to = (1, 2, 1, 2)[n]
+        return remote(
+            usend.at[c, k - 1], urecv.at[c, n], u_send.at[c, n], u_recv.at[c, n], {"dp": flip(d, to)}
+        )
+
+    def scatter(c):
+        for h in range(2):
+            encode(c, 3, h, part[c, 3, h * cr:(h + 1) * cr, :])
+        usend[c, 2] = col[c, 2].T[:8, :]
+        for h in range(2):
+            go(part_copy(c, 3, h, h + 1, h))
+            go(unit_copy(c, 3, h))
+        for k in (1, 2):
+            h = k - 1
+            encode(c, k, h, part[c, k, h * cr:(h + 1) * cr, :])
+            go(part_copy(c, k, h, k, 1 + k))
+
+    def combine(c):
+        for h in range(2):
+            part_copy(c, 3, h, h + 1, h).wait_recv()
+            unit_copy(c, 3, h).wait_recv()
+        lane = lax.broadcasted_iota(jnp.int32, (1, count), 1)
+        unit = jnp.where(lane < cr, urecv[c, 0][0:1, :], urecv[c, 1][0:1, :])
+        ucol = jnp.broadcast_to(unit, (128, count)).T
+        for k in (2, 1):
+            h = 2 - k
+            at = slice(h * cr, (h + 1) * cr)
+            x = part[c, k, at, :] + precv[c, 2, at, :].astype(jnp.int32).astype(F32) * ucol[at, :1]
+            encode(c, k, h, x)
+        for k in (2, 1):
+            usend[c, k - 1] = col[c, k - 1].T[:8, :]
+            go(part_copy(c, k, 2 - k, k, 3 + k))
+            go(unit_copy(c, k, 1 + k))
+
+    column = lax.broadcasted_iota(jnp.int32, (cr, width), 1) + v * width
+    lane = lax.broadcasted_iota(jnp.int32, (cr, 128), 1)
+
+    def stat_copy(c, k):
+        return remote(
+            stats.at[c, v], stats.at[c, v], st_send.at[c, k - 1], st_recv.at[c, k - 1],
+            {"vocab": lax.rem(v + k, nv)},
+        )
+
+    def measure(c):
+        for k in (1, 2):
+            part_copy(c, k, k - 1, k, 1 + k).wait_recv()
+            part_copy(c, k, 2 - k, k, 3 + k).wait_recv()
+            unit_copy(c, k, 1 + k).wait_recv()
+        row = lax.broadcasted_iota(jnp.int32, (128, count), 0)
+        ucol = jnp.where(row == 0, urecv[c, 2][0:1, :], urecv[c, 3][0:1, :]).T
+        for h in range(2):
+            at = slice(h * cr, (h + 1) * cr)
+            natural = slice(h * half + c * cr, h * half + (c + 1) * cr)
+            x = part[c, 0, at, :]
+            for k in (1, 2):
+                x = x + precv[c, k - 1, at, :].astype(jnp.int32).astype(F32) * ucol[at, k - 1:k]
+            top = jnp.max(x, axis=1, keepdims=True)
+            e = jnp.exp(x - top)
+            total = jnp.sum(e, axis=1, keepdims=True)
+            pick = jnp.sum(jnp.where(column == tcol[natural, :1], x, 0.0), axis=1, keepdims=True)
+            part[c, 0, at, :] = e
+            col[c, 0, at, :] = jnp.where(lane == 0, top, jnp.where(lane == 1, total, pick))
+        stats[c, v] = col[c, 0].T[:8, :]
+        for k in range(1, nv):
+            go(stat_copy(c, k))
+
+    def grad_copy(c, k):
+        return remote(
+            grads.at[c, 0], grads.at[c, k], g_send.at[c, k - 1], g_recv.at[c, k - 1], {"dp": flip(d, k)}
+        )
+
+    def differentiate(c):
+        own_top = stats[c, v][0:1, :]
+        for k in range(1, nv):
+            stat_copy(c, k).wait_recv()
+        top = stats[c, 0][0:1, :]
+        for u in range(1, nv):
+            top = jnp.maximum(top, stats[c, u][0:1, :])
+        total = jnp.zeros_like(top)
+        pick = jnp.zeros_like(top)
+        for u in range(nv):
+            block = stats[c, u]
+            total = total + block[1:2, :] * jnp.exp(block[0:1, :] - top)
+            pick = pick + block[2:3, :]
+        loss = top + jnp.log(total) - pick
+        ratio = jnp.exp(own_top - top) / total
+        row = lax.broadcasted_iota(jnp.int32, (128, count), 0)
+        both = jnp.where(row == 0, ratio, loss).T
+        for h in range(2):
+            at = slice(h * cr, (h + 1) * cr)
+            natural = slice(h * half + c * cr, h * half + (c + 1) * cr)
+            losscol[natural, :] = jnp.broadcast_to(both[at, 1:2], (cr, 128))
+            weight = ccol[natural, :1]
+            onehot = jnp.where(column == tcol[natural, :1], weight, 0.0)
+            g = part[c, 0, at, :] * (both[at, :1] * weight) - onehot
+            grads[c, 0, at, :] = g.astype(BF16)
+        for k in (1, 2):
+            go(grad_copy(c, k))
+
+    def relay_copy(c, k):
+        at = pl.ds((k - 1) * cr, cr)
+        return remote(
+            grads.at[c, k, at], grads.at[c, 3, at], r_send.at[c, k - 1], r_recv.at[c, k - 1], {"dp": flip(d, 3 - k)}
+        )
+
+    def relay(c):
+        for k in (1, 2):
+            grad_copy(c, k).wait_recv()
+            go(relay_copy(c, k))
+
+    depth_tile = min(256, depth)
+    chunk_rows = min(16, cr)
+
+    def mate_sum(c):
+        return remote(xsend.at[c], xrecv.at[c], x_send.at[c], x_recv.at[c], {"vocab": mate})
+
+    def pull(c):
+        for k in (1, 2):
+            relay_copy(c, k).wait_recv()
+
+        def step(n, _):
+            at = pl.ds(pl.multiple_of(n * depth_tile, depth_tile), depth_tile)
+            value = lax.dot_general(
+                grads[c].reshape(total_rows, width), w[at, :], (((1,), (1,)), ((), ())),
+                preferred_element_type=F32,
+            )
+            acc[c, :, :, :, at] = value.reshape(nd, 2, cr, depth_tile)
+            return 0
+
+        lax.fori_loop(0, depth // depth_tile, step, 0)
+
+        def cast(k, _):
+            for i in range(cr // chunk_rows):
+                at = slice(i * chunk_rows, (i + 1) * chunk_rows)
+                xsend[c, k, at, :] = acc[c, k, 1 - core, at, :].astype(BF16)
+            return 0
+
+        lax.fori_loop(0, nd, cast, 0)
+        go(mate_sum(c))
+
+    far = jnp.where(2 * z < chips, chips - 1, 0)
+    near_end = jnp.logical_or(z == 0, z == chips - 1)
+    goals = []
+    for j in range(chips - 1):
+        inner = jnp.where(2 * z < chips, jnp.where(z == 0, chips - 1 - j, (3, 0, 2)[j]), jnp.where(z == chips - 1, j, (0, 3, 1)[j]))
+        goals.append(inner)
+    goals.append(z)
+
+    def chain_copy(c, j, goal):
+        back = jnp.where(goal < z, 1, 0)
+        return remote(
+            zsend.at[c, j], zrecv.at[back, c, goal], z_send.at[c, j], z_recv.at[back, c, goal],
+            {"vocab": v + 2 - 4 * back},
+        )
+
+    def each(body):
+        def step(i, _):
+            body(pl.ds(pl.multiple_of(i * chunk_rows, chunk_rows), chunk_rows))
+            return 0
+
+        lax.fori_loop(0, cr // chunk_rows, step, 0)
+
+    def exchange(c):
+        mate_sum(c).wait_recv()
+
+    def forward(c, j):
+        goal = goals[j]
+        k = xor(d, goal)
+        back = jnp.where(goal < z, 1, 0)
+
+        @pl.when(near_end)
+        def _():
+            def first(at):
+                zsend[c, j, at, :] = (acc[c, k, core, at, :] + xrecv[c, k, at, :].astype(F32)).astype(BF16)
+
+            each(first)
+
+        @pl.when(jnp.logical_not(near_end))
+        def _():
+            chain_copy(c, j, goal).wait_recv()
+
+            def add(at):
+                zsend[c, j, at, :] = (
+                    acc[c, k, core, at, :] + xrecv[c, k, at, :].astype(F32) + zrecv[back, c, goal, at, :].astype(F32)
+                ).astype(BF16)
+
+            each(add)
+
+        chain_copy(c, j, goal).start()
+
+    def arrive(c, back):
+        return remote(zsend.at[c, 0], zrecv.at[back, c, z], z_send.at[c, 0], z_recv.at[back, c, z], {"vocab": mate})
+
+    def finish(c):
+        k = xor(d, z)
+        back = jnp.where(z == 0, 1, 0)
+
+        def there(at):
+            return pl.ds(pl.multiple_of(c * cr + at.start, chunk_rows), chunk_rows)
+
+        @pl.when(near_end)
+        def _():
+            arrive(c, back).wait_recv()
+
+            def add(at):
+                gh_ref[there(at), :] = (
+                    acc[c, k, core, at, :] + xrecv[c, k, at, :].astype(F32) + zrecv[back, c, z, at, :].astype(F32)
+                ).astype(BF16)
+
+            each(add)
+
+        @pl.when(jnp.logical_not(near_end))
+        def _():
+            arrive(c, 0).wait_recv()
+            arrive(c, 1).wait_recv()
+
+            def add(at):
+                gh_ref[there(at), :] = (
+                    acc[c, k, core, at, :] + xrecv[c, k, at, :].astype(F32)
+                    + zrecv[0, c, z, at, :].astype(F32) + zrecv[1, c, z, at, :].astype(F32)
+                ).astype(BF16)
+
+            each(add)
+
+    def weigh(n):
+        at = pl.ds(n * depth_tile, depth_tile)
+        gw_ref[at, :] = lax.dot_general(
+            spread[:, :, :, at].reshape(chunks * total_rows, depth_tile),
+            grads[...].reshape(chunks * total_rows, width),
+            (((0,), (0,)), ((), ())), preferred_element_type=F32,
+        ).astype(BF16)
+
+    steps = {
+        "a": gather, "b": cross, "p": project, "s": scatter, "r": combine, "m": measure, "g": differentiate,
+        "l": relay, "u": pull, "x": exchange, "f": finish, "w": weigh,
+    }
+    for name in plan:
+        if name[0] == "y":
+            forward(int(name[1]), int(name[2]))
+        else:
+            steps[name[0]](int(name[1]))
+
+    loss_ref[...] = losscol[...].T[:1, :]
+    for copy in sent:
+        copy.wait_send()
+    for c in range(chunks):
+        for j, goal in enumerate(goals[:-1]):
+            chain_copy(c, j, goal).wait_send()
+
+
+PLAN = (
+    "a0", "a1", "b0", "a2", "p0", "b1", "s0", "a3", "p1", "r0", "b2", "s1", "p2", "s2",
+    "r1", "m0", "r2", "b3", "g0", "p3", "m1", "s3", "m2", "l0", "r3", "g1", "g2", "m3",
+    "u0", "l1", "g3", "l2", "x0", "y00", "y01", "y02", "u1", "l3", "u2", "x1", "y10", "u3",
+    "x2", "y20", "y11", "x3", "y30", "y12", "w2", "w5", "w7", "w1", "w6", "y21", "w3", "y31",
+    "y22", "w4", "f0", "w0", "f1", "y32", "f2", "f3",
+)
+
+
+def chain(nd, nv, hidden, weight, targets, cotangent):
+    rows = hidden.shape[0]
+    tokens = rows * nd
+    depth, width = weight.shape
+    share = tokens // nv
+    chips = nv // 2
+    cr = rows // 2 // CHUNKS
+    count = 2 * cr
+    dma = pltpu.SemaphoreType.DMA
+    vmem = pl.BlockSpec(memory_space=pltpu.VMEM)
+    anywhere = pl.BlockSpec(memory_space=pl.ANY)
+    flops = 6 * tokens * depth * width
+
+    def both(*shape):
+        return [dma(shape), dma(shape)]
+
+    loss, grad_hidden, grad_weight = pl.pallas_call(
+        functools.partial(chain_kernel, nd, nv, PLAN),
+        out_shape=(
+            pltpu.VMEM((1, rows), F32),
+            pltpu.VMEM((share, depth), BF16),
+            pltpu.VMEM((depth, width), BF16),
+        ),
+        in_specs=[anywhere, anywhere, vmem, vmem],
+        out_specs=(vmem, vmem, vmem),
+        scratch_shapes=[
+            pltpu.VMEM((depth, width), BF16),
+            pltpu.VMEM((CHUNKS, nd, count, depth), BF16),
+            pltpu.VMEM((CHUNKS, nd, count, width), F32),
+            pltpu.VMEM((CHUNKS, nd - 1, count, width), WIRE),
+            pltpu.VMEM((CHUNKS, nd - 1, count, width), WIRE),
+            pltpu.VMEM((CHUNKS, nd - 1, 8, count), F32),
+            pltpu.VMEM((CHUNKS, 4, 8, count), F32),
+            pltpu.VMEM((CHUNKS, nv, 8, count), F32),
+            pltpu.VMEM((CHUNKS, nd, count, width), BF16),
+            pltpu.VMEM((CHUNKS, nd, 2, cr, depth), F32),
+            pltpu.VMEM((CHUNKS, nd, cr, depth), BF16),
+            pltpu.VMEM((CHUNKS, nd, cr, depth), BF16),
+            pltpu.VMEM((CHUNKS, chips - 1, cr, depth), BF16),
+            pltpu.VMEM((2, CHUNKS, chips, cr, depth), BF16),
+            pltpu.VMEM((rows, 128), jnp.int32),
+            pltpu.VMEM((rows, 128), F32),
+            pltpu.VMEM((CHUNKS, nd - 1, count, 128), F32),
+            pltpu.VMEM((rows, 128), F32),
+            dma, dma((CHUNKS, 2)),
+            *both(CHUNKS, nd - 1), *both(CHUNKS), *both(CHUNKS, 2), *both(CHUNKS, 6), *both(CHUNKS, 4),
+            *both(CHUNKS, nv - 1), *both(CHUNKS, 2), *both(CHUNKS, 2), *both(CHUNKS),
+            dma((CHUNKS, chips - 1)), dma((2, CHUNKS, chips)),
+        ],
+        compiler_params=pltpu.CompilerParams(
+            collective_id=0, has_side_effects=True, vmem_limit_bytes=VMEM_GRANT
+        ),
+        cost_estimate=pl.CostEstimate(flops=flops, bytes_accessed=16 << 20, transcendentals=0),
+        name="token_loss",
+    )(hidden, weight, targets.reshape(1, rows), cotangent.reshape(1, rows))
+    return loss.reshape(rows), grad_hidden, grad_weight
+
+
 def solution(mesh):
     in_specs = (P("dp", None), P("dp", "vocab"), P("dp"), P("dp"))
     out_specs = (P("dp"), P("vocab", "dp"), P("dp", "vocab"))
-    body = functools.partial(shards, mesh.shape["dp"], mesh.shape["vocab"])
+    nd, nv = mesh.shape["dp"], mesh.shape["vocab"]
+    form = chain if nd == 4 and nv == 2 * nd else butterfly
+    body = functools.partial(form, nd, nv)
     return jax.shard_map(body, mesh=mesh, in_specs=in_specs, out_specs=out_specs, check_vma=False)

time: 123 us -> 93.9 us (0.76)
  the two profiles are of different devices: /device:TPU:7 before, /device:TPU:0 now
where the time goes in v1:
time: 93.9 us; the launch traced here: 93.7 us
  Pallas kernels  89.7 us (96%)
  local copies, waits for them, and re-layouts  3.37 us (4%)
    pallas_call x1, Pallas kernels, chain(): pl.pallas_call(functools.partial(chain_kernel, nd, nv, PLAN), out_shape=(...  89.7 us
    unnamed x3, local copies, waits for them, and re-layouts  3.37 us

profile of v1, /device:TPU:0, one launch (start us, length us, event | category | flops | bytes accessed | tf_op | source)
XLA Modules:
  0.0 93.7 jit_solution(16058670753501922987)
XLA Ops:
  0.6 89.7 %token_loss.1 = (f32[1,256]{1,0:T(1,128)S(1)}, bf16[128,2048]{1,0:T(8,128)(2,1)S(1)}, bf16[2048,1024]{1,0:T(8,128)(2,1)S(1)}) custom-call(bf16[256,8192]{1,0:T(8,128)(2,1)} %h_ref.1, bf16[2048,1024]{1,0:T(8,128)(2,1)} %w_hbm.1, s32[1,256]{1,0:T(1,128)} %bitcast.4, f32[1,256]{1,0:T(1,128)} %bitcast.5), custom_call_target="tpu_custom_call" | custom-call | flops 12884901888 | bytes 16777216 | tf_op jit(solution)/shard_map/token_loss/pallas_call | solution.py:830
  90.3 0.6 copy.10
  90.9 0.8 copy.11
  91.7 2.0 %copy.12 = bf16[2048,1024]{1,0:T(8,128)(2,1)} copy(bf16[2048,1024]{1,0:T(8,128)(2,1)S(1)} %get-tuple-element.11) | data formatting | bytes 8388608
